TPU v7x, 256 devices: a whole 4x4x8 slice. The times are simulated.
256 devices in a mesh: grp: 4 (over y), mem: 64 (over z, x, core).
Axes of the slice: x: 4, y: 4, z: 8, core: 2. Of those that a mesh axis runs over, the one named last changes fastest.
Arguments:
- values: bfloat16 [256, 64, 32, 128], P(('grp', 'mem')), may hold values from -6 to 6
- slots: int32 [256, 64, 32], P(('grp', 'mem')), may hold values from 0 to 7167
- counts: int32 [256, 64], P(('grp', 'mem')), may hold values from 0 to 32, as said below
Outputs:
- averaged: float32 [458752, 128], P('mem')
- returned: bfloat16 [256, 64, 32, 128], P(('grp', 'mem'))
Inputs may be any that keep to these rules, and one draw needn't show every extreme that they name: `counts`: every device has at least one list with exactly 32 valid entries.
All inputs are finite; a program needn't handle non-finite values.
Results may differ from a plain program's by a relative error of at most 0.0024.
Values may be sent and summed in bfloat16 or wider, within the bound.
A program may use at most 64 MiB of HBM per device.

v0:
```python
import math

import jax
import jax.numpy as jnp
from jax import lax
from jax.sharding import PartitionSpec as P

BUCKET = 7168


def split_up(shard, dim, peers):
    shape = shard.shape
    pieces = shard.reshape(*shape[:dim], peers, shape[dim] // peers, *shape[dim + 1 :])
    return jnp.moveaxis(pieces, dim, 0)


def summed_on_arrival(shard, axis, dim):
    peers = lax.axis_size(axis)
    pieces = lax.all_to_all(split_up(shard, dim, peers), axis, 0, 0, tiled=True)
    return jnp.sum(pieces, axis=0)


def laid_out(pieces, dim):
    pieces = jnp.moveaxis(pieces, 0, dim)
    shape = pieces.shape
    return pieces.reshape(*shape[:dim], shape[dim] * shape[dim + 1], *shape[dim + 2 :])


def from_everyone(shard, axis):
    peers = lax.axis_size(axis)
    return lax.all_to_all(
        jnp.broadcast_to(shard[None], (peers, *shard.shape)), axis, 0, 0, tiled=True
    )


def gathered_copies(shard, axis, dim):
    return laid_out(from_everyone(shard, axis), dim)


def tiled_sums(rows_in, slot_in):
    lane_count = rows_in.shape[1]
    tile = math.gcd(BUCKET, 1024)

    def one_tile(first):
        wanted = first + lax.broadcasted_iota(jnp.int32, (tile, 1), 0)
        onehot = (wanted == slot_in[None, :]).astype(jnp.bfloat16)
        return jnp.dot(onehot, rows_in, preferred_element_type=jnp.float32)

    starts = jnp.arange(BUCKET // tile, dtype=jnp.int32) * tile
    return lax.map(one_tile, starts).reshape(BUCKET, lane_count)


def live_counts(slot_in):
    live_in = (slot_in >= 0).astype(jnp.float32)
    return jax.ops.segment_sum(live_in, jnp.maximum(slot_in, 0), num_segments=BUCKET)


def per_device(values, slots, counts):
    blocks_out = values[0]
    slot_ids = slots[0]
    list_counts = counts[0]
    members, capacity, lane_count = blocks_out.shape
    is_valid = lax.broadcasted_iota(jnp.int32, (members, capacity), 1) < list_counts[:, None]
    send_blocks = jnp.where(is_valid[:, :, None], blocks_out, jnp.zeros_like(blocks_out))
    send_slots = jnp.where(is_valid, slot_ids, -1)
    got_blocks, got_slots = (
        lax.all_to_all(send_blocks, "mem", split_axis=0, concat_axis=0, tiled=True),
        lax.all_to_all(send_slots, "mem", split_axis=0, concat_axis=0, tiled=True),
    )
    rows_in = got_blocks.reshape(members * capacity, lane_count)
    slot_in = got_slots.reshape(members * capacity)
    slot_count = None
    local_sums = tiled_sums(rows_in, slot_in)
    payload = (local_sums, live_counts(slot_in))
    reduced = jax.tree.map(lambda part: summed_on_arrival(part, "grp", 0), payload)
    share = BUCKET // lax.axis_size("grp")
    share_count = reduced[1]
    share_mean = reduced[0] / jnp.maximum(share_count, 1.0)[:, None]
    averaged = gathered_copies(share_mean.astype(jnp.bfloat16), "grp", 0).astype(share_mean.dtype)
    owned_rows = jnp.take(averaged, jnp.maximum(slot_in, 0), axis=0)
    back_rows = jnp.where((slot_in >= 0)[:, None], owned_rows, 0.0).astype(jnp.bfloat16)
    back_rows = back_rows.reshape(members, capacity, lane_count)
    returned = lax.all_to_all(back_rows, "mem", split_axis=0, concat_axis=0, tiled=True)
    return (averaged, returned[None])


def solution(mesh):
    return jax.shard_map(
        per_device,
        mesh=mesh,
        in_specs=(
            P(("grp", "mem"), None, None, None),
            P(("grp", "mem"), None, None),
            P(("grp", "mem"), None),
        ),
        out_specs=(P("mem", None), P(("grp", "mem"), None, None, None)),
        check_vma=False,
    )
```

profile of v0, /device:TPU:1, one launch (start us, length us, event | category | flops | bytes accessed | tf_op | source)
XLA Modules:
  0.0 189.3 jit_solution(9789190772218679304)
XLA Ops:
  0.6 0.8 copy.9
  1.4 1.4 compare_select_fusion
  2.8 13.0 %all-to-all-start = ((s32[64,1,32]{2,1,0:T(1,128)}), s32[64,1,32]{2,1,0:T(1,128)S(1)}, u32[]{:S(2)}, u32[]{:S(2)}) async-start(s32[64,1,32]{2,1,0:T(1,128)} %compare_select_fusion), calls=%async_computation | async-start | bytes 65536 | tf_op jit(solution)/shard_map/all_to_all | solution.py:68
  15.8 0.7 iota_compare_fusion
  16.6 2.2 %bitcast_select_fusion = bf16[64,32,128]{2,1,0:T(8,128)(2,1)} fusion(bf16[1,64,32,128]{3,2,1,0:T(8,128)(2,1)} %param.5, pred[64,32]{1,0:T(8,128)(4,1)S(1)} %iota_compare_fusion), kind=kLoop, calls=%fused_computation.12 | loop fusion | flops 262144 | bytes 1050624 | tf_op jit(solution)/shard_map/jit(_where)/select_n | solution.py:64
  18.7 6.4 %all-to-all-done = s32[64,1,32]{2,1,0:T(1,128)S(1)} async-done(((s32[64,1,32]{2,1,0:T(1,128)}), s32[64,1,32]{2,1,0:T(1,128)S(1)}, u32[]{:S(2)}, u32[]{:S(2)}) %all-to-all-start) | async-done | bytes 8224 | tf_op jit(solution)/shard_map/all_to_all | solution.py:68
  25.1 4.7 %all-to-all-start.1 = ((bf16[64,32,128]{2,1,0:T(8,128)(2,1)}), bf16[64,32,128]{2,1,0:T(8,128)(2,1)S(1)}, u32[]{:S(2)}, u32[]{:S(2)}) async-start(bf16[64,32,128]{2,1,0:T(8,128)(2,1)} %bitcast_select_fusion), calls=%async_computation.1 | async-start | bytes 1048576 | tf_op jit(solution)/shard_map/all_to_all | solution.py:67
  30.3 12.4 %scatter_custom_fusion = f32[7168]{0:T(1024)} fusion(s32[2048]{0:T(1024)S(1)} %reshape.167, f32[2048]{0:T(1024)S(1)} %reshape.169, f32[]{:T(128)} %constant.16.clone.1), kind=kCustom, calls=%fused_computation.20 | custom fusion | flops 2048 | bytes 28676 | tf_op jit(solution)/shard_map/scatter-add | solution.py:55
  42.8 4.9 %all-to-all-done.1 = bf16[64,32,128]{2,1,0:T(8,128)(2,1)S(1)} async-done(((bf16[64,32,128]{2,1,0:T(8,128)(2,1)}), bf16[64,32,128]{2,1,0:T(8,128)(2,1)S(1)}, u32[]{:S(2)}, u32[]{:S(2)}) %all-to-all-start.1) | async-done | bytes 524320 | tf_op jit(solution)/shard_map/all_to_all | solution.py:67
  47.7 4.2 %all-to-all-start.3 = ((f32[4,1,1792]{2,1,0:T(1,128)}), f32[4,1,1792]{2,1,0:T(1,128)S(1)}, u32[]{:S(2)}, u32[]{:S(2)}) async-start(f32[4,1,1792]{2,1,0:T(1,128)} %bitcast.8), calls=%async_computation.3 | async-start | bytes 57344 | tf_op jit(solution)/shard_map/all_to_all | solution.py:19
  51.9 23.4 %while.11 = (s32[]{:T(128)}, f32[7,1024,128]{2,1,0:T(8,128)}, s32[7]{0:T(128)S(1)}, s32[64,32]{1,0:T(8,128)}, bf16[2048,128]{1,0:T(8,128)(2,1)S(1)}, /*index=5*/s32[2048]{0:T(1024)S(1)}, s32[]{:T(128)}) while((s32[]{:T(128)}, f32[7,1024,128]{2,1,0:T(8,128)}, s32[7]{0:T(128)S(1)}, s32[64,32]{1,0:T(8,128)}, ...), condition=%wide.wide.region_1.2_spmd, body=%wide.wide.region_0.1_spmd.sunk | while | flops 538969088 | bytes 1065565 | solution.py:50
  52.5 0.6 iota_add_fusion.3
  53.1 2.1 %fusion.22 = f32[7,1024,128]{2,1,0:T(8,128)} fusion(f32[7,1024,128]{2,1,0:T(8,128)} %get-tuple-element.107, s32[]{:T(128)} %get-tuple-element.106, bf16[2048,128]{1,0:T(8,128)(2,1)S(1)} %get-tuple-element.117, s32[2048]{0:T(1024)S(1)} %get-tuple-element.118, s32[1024]{0:T(1024)S(1)} %iota_add_fusion.3), kind=kOutput, calls=%fused_computation.7.clone.clone.1 | convolution fusion | flops 538968064 | bytes 1061376 | tf_op jit(solution)/shard_map/while/body/eval_jaxpr/dot_general | solution.py:47
  55.8 0.6 iota_add_fusion.3
  56.5 2.1 %fusion.22 = f32[7,1024,128]{2,1,0:T(8,128)} fusion(f32[7,1024,128]{2,1,0:T(8,128)} %get-tuple-element.107, s32[]{:T(128)} %get-tuple-element.106, bf16[2048,128]{1,0:T(8,128)(2,1)S(1)} %get-tuple-element.117, s32[2048]{0:T(1024)S(1)} %get-tuple-element.118, s32[1024]{0:T(1024)S(1)} %iota_add_fusion.3), kind=kOutput, calls=%fused_computation.7.clone.clone.1 | convolution fusion | flops 538968064 | bytes 1061376 | tf_op jit(solution)/shard_map/while/body/eval_jaxpr/dot_general | solution.py:47
  59.8 2.1 %fusion.22 = f32[7,1024,128]{2,1,0:T(8,128)} fusion(f32[7,1024,128]{2,1,0:T(8,128)} %get-tuple-element.107, s32[]{:T(128)} %get-tuple-element.106, bf16[2048,128]{1,0:T(8,128)(2,1)S(1)} %get-tuple-element.117, s32[2048]{0:T(1024)S(1)} %get-tuple-element.118, s32[1024]{0:T(1024)S(1)} %iota_add_fusion.3), kind=kOutput, calls=%fused_computation.7.clone.clone.1 | convolution fusion | flops 538968064 | bytes 1061376 | tf_op jit(solution)/shard_map/while/body/eval_jaxpr/dot_general | solution.py:47
  63.2 2.1 %fusion.22 = f32[7,1024,128]{2,1,0:T(8,128)} fusion(f32[7,1024,128]{2,1,0:T(8,128)} %get-tuple-element.107, s32[]{:T(128)} %get-tuple-element.106, bf16[2048,128]{1,0:T(8,128)(2,1)S(1)} %get-tuple-element.117, s32[2048]{0:T(1024)S(1)} %get-tuple-element.118, s32[1024]{0:T(1024)S(1)} %iota_add_fusion.3), kind=kOutput, calls=%fused_computation.7.clone.clone.1 | convolution fusion | flops 538968064 | bytes 1061376 | tf_op jit(solution)/shard_map/while/body/eval_jaxpr/dot_general | solution.py:47
  66.5 2.1 %fusion.22 = f32[7,1024,128]{2,1,0:T(8,128)} fusion(f32[7,1024,128]{2,1,0:T(8,128)} %get-tuple-element.107, s32[]{:T(128)} %get-tuple-element.106, bf16[2048,128]{1,0:T(8,128)(2,1)S(1)} %get-tuple-element.117, s32[2048]{0:T(1024)S(1)} %get-tuple-element.118, s32[1024]{0:T(1024)S(1)} %iota_add_fusion.3), kind=kOutput, calls=%fused_computation.7.clone.clone.1 | convolution fusion | flops 538968064 | bytes 1061376 | tf_op jit(solution)/shard_map/while/body/eval_jaxpr/dot_general | solution.py:47
  69.2 0.6 iota_add_fusion.3
  69.9 2.1 %fusion.22 = f32[7,1024,128]{2,1,0:T(8,128)} fusion(f32[7,1024,128]{2,1,0:T(8,128)} %get-tuple-element.107, s32[]{:T(128)} %get-tuple-element.106, bf16[2048,128]{1,0:T(8,128)(2,1)S(1)} %get-tuple-element.117, s32[2048]{0:T(1024)S(1)} %get-tuple-element.118, s32[1024]{0:T(1024)S(1)} %iota_add_fusion.3), kind=kOutput, calls=%fused_computation.7.clone.clone.1 | convolution fusion | flops 538968064 | bytes 1061376 | tf_op jit(solution)/shard_map/while/body/eval_jaxpr/dot_general | solution.py:47
  73.2 2.1 %fusion.22 = f32[7,1024,128]{2,1,0:T(8,128)} fusion(f32[7,1024,128]{2,1,0:T(8,128)} %get-tuple-element.107, s32[]{:T(128)} %get-tuple-element.106, bf16[2048,128]{1,0:T(8,128)(2,1)S(1)} %get-tuple-element.117, s32[2048]{0:T(1024)S(1)} %get-tuple-element.118, s32[1024]{0:T(1024)S(1)} %iota_add_fusion.3), kind=kOutput, calls=%fused_computation.7.clone.clone.1 | convolution fusion | flops 538968064 | bytes 1061376 | tf_op jit(solution)/shard_map/while/body/eval_jaxpr/dot_general | solution.py:47
  75.3 4.7 %all-to-all-start.2 = ((f32[4,1792,128]{2,1,0:T(8,128)}), f32[4,1792,128]{2,1,0:T(8,128)}, u32[]{:S(2)}, u32[]{:S(2)}) async-start(f32[4,1792,128]{2,1,0:T(8,128)} %bitcast.28), calls=%async_computation.2 | async-start | bytes 7340032 | tf_op jit(solution)/shard_map/all_to_all | solution.py:19
  80.1 42.5 %all-to-all-done.2 = f32[4,1792,128]{2,1,0:T(8,128)} async-done(((f32[4,1792,128]{2,1,0:T(8,128)}), f32[4,1792,128]{2,1,0:T(8,128)}, u32[]{:S(2)}, u32[]{:S(2)}) %all-to-all-start.2) | async-done | bytes 3670048 | tf_op jit(solution)/shard_map/all_to_all | solution.py:19
  122.7 2.3 %reduce_sum.18 = f32[1792,128]{1,0:T(8,128)S(1)} reduce(f32[4,1792,128]{2,1,0:T(8,128)} %all-to-all-done.2, f32[]{:T(128)} %constant.16.clone.1), dimensions={0}, to_apply=%region_2.3 | reduce | flops 688128 | bytes 4587524 | tf_op jit(solution)/shard_map/reduce_sum | solution.py:20
  125.3 1.5 broadcast_in_dim.65
  126.8 3.6 %all-to-all-start.4 = ((bf16[4,1792,128]{2,1,0:T(8,128)(2,1)}), bf16[4,1792,128]{2,1,0:T(8,128)(2,1)S(1)}, u32[]{:S(2)}, u32[]{:S(2)}) async-start(bf16[4,1792,128]{2,1,0:T(8,128)(2,1)} %broadcast_in_dim.65), calls=%async_computation.4 | async-start | bytes 3670016 | tf_op jit(solution)/shard_map/all_to_all | solution.py:31
  130.4 21.9 %all-to-all-done.4 = bf16[4,1792,128]{2,1,0:T(8,128)(2,1)S(1)} async-done(((bf16[4,1792,128]{2,1,0:T(8,128)(2,1)}), bf16[4,1792,128]{2,1,0:T(8,128)(2,1)S(1)}, u32[]{:S(2)}, u32[]{:S(2)}) %all-to-all-start.4) | async-done | bytes 1835040 | tf_op jit(solution)/shard_map/all_to_all | solution.py:31
  152.4 2.2 %bitcast_convert_fusion = f32[7168,128]{1,0:T(8,128)} fusion(bf16[4,1792,128]{2,1,0:T(8,128)(2,1)S(1)} %all-to-all-done.4), kind=kLoop, calls=%fused_computation.9 | loop fusion | flops 917504 | bytes 5505024 | tf_op jit(solution)/shard_map/convert_element_type | solution.py:79
  154.6 7.6 %gather_fusion = bf16[2048,128]{1,0:T(8,128)(2,1)S(1)} fusion(f32[7168,128]{1,0:T(8,128)} %bitcast_convert_fusion, s32[2048]{0:T(1024)S(1)} %broadcast_clamp_fusion), kind=kCustom, calls=%fused_computation | custom fusion | bytes 1056768 | tf_op jit(solution)/shard_map/jit(_take)/gather | solution.py:80
  162.2 0.7 select_convert_fusion
  162.9 25.6 %all_to_all.38 = bf16[64,32,128]{2,1,0:T(8,128)(2,1)S(1)} all-to-all(bf16[64,32,128]{2,1,0:T(8,128)(2,1)S(1)} %select_convert_fusion), channel_id=1, replica_groups=mesh['grp'=4,'mem'=64] {'mem'}, dimensions={0} | all-to-all | bytes 1048576 | tf_op jit(solution)/shard_map/all_to_all | solution.py:83
  188.5 0.8 copy.22
  (28 shorter events, 7.5 us)
Async XLA Ops:
  2.8 22.3 %all-to-all-start = ((s32[64,1,32]{2,1,0:T(1,128)}), s32[64,1,32]{2,1,0:T(1,128)S(1)}, u32[]{:S(2)}, u32[]{:S(2)}) async-start(s32[64,1,32]{2,1,0:T(1,128)} %compare_select_fusion), calls=%async_computation | async-start | bytes 65536 | tf_op jit(solution)/shard_map/all_to_all | solution.py:68
  25.1 26.7 %copy-start = (s32[64,1,32]{2,1,0:T(1,128)}, s32[64,1,32]{2,1,0:T(1,128)S(1)}, u32[]{:S(2)}) copy-start(s32[64,1,32]{2,1,0:T(1,128)S(1)} %all-to-all-done) | copy-start | bytes 24580
  25.1 22.6 %all-to-all-start.1 = ((bf16[64,32,128]{2,1,0:T(8,128)(2,1)}), bf16[64,32,128]{2,1,0:T(8,128)(2,1)S(1)}, u32[]{:S(2)}, u32[]{:S(2)}) async-start(bf16[64,32,128]{2,1,0:T(8,128)(2,1)} %bitcast_select_fusion), calls=%async_computation.1 | async-start | bytes 1048576 | tf_op jit(solution)/shard_map/all_to_all | solution.py:67
  47.7 27.6 %all-to-all-start.3 = ((f32[4,1,1792]{2,1,0:T(1,128)}), f32[4,1,1792]{2,1,0:T(1,128)S(1)}, u32[]{:S(2)}, u32[]{:S(2)}) async-start(f32[4,1,1792]{2,1,0:T(1,128)} %bitcast.8), calls=%async_computation.3 | async-start | bytes 57344 | tf_op jit(solution)/shard_map/all_to_all | solution.py:19
  75.3 47.3 %all-to-all-start.2 = ((f32[4,1792,128]{2,1,0:T(8,128)}), f32[4,1792,128]{2,1,0:T(8,128)}, u32[]{:S(2)}, u32[]{:S(2)}) async-start(f32[4,1792,128]{2,1,0:T(8,128)} %bitcast.28), calls=%async_computation.2 | async-start | bytes 7340032 | tf_op jit(solution)/shard_map/all_to_all | solution.py:19
  125.0 5.4 %copy-start.1 = (s32[64,32]{1,0:T(8,128)S(1)}, s32[64,32]{1,0:T(8,128)}, u32[]{:S(2)}) copy-start(s32[64,32]{1,0:T(8,128)} %get-tuple-element.128) | copy-start | bytes 24580
  126.8 25.6 %all-to-all-start.4 = ((bf16[4,1792,128]{2,1,0:T(8,128)(2,1)}), bf16[4,1792,128]{2,1,0:T(8,128)(2,1)S(1)}, u32[]{:S(2)}, u32[]{:S(2)}) async-start(bf16[4,1792,128]{2,1,0:T(8,128)(2,1)} %broadcast_in_dim.65), calls=%async_computation.4 | async-start | bytes 3670016 | tf_op jit(solution)/shard_map/all_to_all | solution.py:31
where the time goes:
time: 191 us; the launch traced here: 189 us
  waiting for transfers between devices  75.8 us (40%)
  starting transfers between devices  30.2 us (16%)
  other arithmetic  27.1 us (14%)
  blocking collectives  25.6 us (13%)
  local copies, waits for them, and re-layouts  15 us (8%)
  matrix products  14.8 us (8%)
    all_to_all x2, waiting for transfers between devices, summed_on_arrival(): pieces = lax.all_to_all(split_up(shard, dim, peers), axis, 0, 0, tiled=True)  42.5 us
    all_to_all x1, blocking collectives, per_device(): lax.all_to_all(back_rows, 'mem', split_axis=0, concat_axis=0, tiled=True)  25.6 us
    all_to_all x1, waiting for transfers between devices, from_everyone(): lax.all_to_all(jnp.broadcast_to(shard[None], (peers, *shard.shape)), axis...  21.9 us
    dot_general x7, matrix products, one_tile(): return jnp.dot(onehot, rows_in, preferred_element_type=jnp.float32)  14.8 us
    all_to_all x1, starting transfers between devices, per_device(): lax.all_to_all(send_slots, 'mem', split_axis=0, concat_axis=0, tiled=True)  13 us
    scatter-add x1, other arithmetic, live_counts(): jax.ops.segment_sum(live_in, jnp.maximum(slot_in, 0), num_segments=BUCKET)  12.4 us
    all_to_all x2, starting transfers between devices, summed_on_arrival(): pieces = lax.all_to_all(split_up(shard, dim, peers), axis, 0, 0, tiled=True)  8.93 us
    gather x1, local copies, waits for them, and re-layouts, per_device(): owned_rows = jnp.take(averaged, jnp.maximum(slot_in, 0), axis=0)  7.62 us
  transfers between devices with their start and end apart: 5, of which 4 were waited for; matrix products, arithmetic and copies ran while one was open for 21% of the time, Pallas kernels for 0%

commit v1 on v0

v1 whole, which is shorter than its diff:
```python
import functools

import jax
import jax.numpy as jnp
from jax import lax
from jax.experimental import pallas as pl
from jax.experimental.pallas import tpu as pltpu
from jax.sharding import PartitionSpec as P

MESH = pl.DeviceIdType.MESH

GROUPS = 4
MEMBERS = 64
CAP = 32
BLOCK = 128
BUCKET = 7168
HALF = BUCKET // 2
PER_CHUNK = 8
CHUNKS = MEMBERS // PER_CHUNK
PAIR = 2 * PER_CHUNK
PIECE = PAIR * CAP
PIECES = MEMBERS // PAIR


def z_step(chunk):
    odd = chunk % 2
    return odd * ((chunk + 1) // 2) + (1 - odd) * ((8 - chunk // 2) % 8)


def member_at(me, chunk, place, sign):
    z, x, core = me // 8, (me // 2) % 4, me % 2
    z_to = (z + 8 + sign * z_step(chunk)) % 8
    x_to = (x + 4 + sign * (place // 2)) % 4
    core_to = (core + place) % 2
    return z_to * 8 + x_to * 2 + core_to


def lanes(shape):
    return lax.broadcasted_iota(jnp.int32, shape, len(shape) - 1)


def in_half(slot):
    return jnp.where(slot >= HALF, slot - HALF, slot)


def kernel(
    values, slots, counts, averaged_out, returned_out,
    vals, raw_slots, raw_counts, sent_slots, rows, row_slots, flat, lane_slots, wide_slots,
    sums, tally, mean, averaged, back,
    load_sem, out_sem, send_sem, own_sem, ring_sem, slot_sem, back_sem,
):
    group = lax.axis_index("grp")
    me = lax.axis_index("mem")
    up, down = (group + 1) % GROUPS, (group + GROUPS - 1) % GROUPS

    barrier = pltpu.get_barrier_semaphore()

    def greet(k, _):
        to = member_at(me, k // PER_CHUNK, k % PER_CHUNK, 1)
        pl.semaphore_signal(barrier, inc=1, device_id={"grp": group, "mem": to}, device_id_type=MESH)
        return 0

    lax.fori_loop(1, MEMBERS, greet, 0)
    for other in (up, down):
        pl.semaphore_signal(barrier, inc=1, device_id={"grp": other, "mem": me}, device_id_type=MESH)

    load_slots = pltpu.make_async_copy(slots.at[0], raw_slots, load_sem.at[0])
    load_counts = pltpu.make_async_copy(counts, raw_counts, load_sem.at[1])
    load_values = pltpu.make_async_copy(values.at[0], vals, load_sem.at[2])
    load_own = pltpu.make_async_copy(values.at[0, me], rows.at[0, 0], load_sem.at[3])
    load_slots.start()
    load_counts.start()
    load_values.start()
    load_own.start()

    load_slots.wait()
    load_counts.wait()
    square = (MEMBERS, MEMBERS)
    on_diagonal = lax.broadcasted_iota(jnp.int32, square, 0) == lanes(square)
    spread = jnp.broadcast_to(raw_counts[...], square)
    count_column = jnp.sum(jnp.where(on_diagonal, spread, 0).astype(jnp.float32), axis=1, keepdims=True)
    count_column = count_column.astype(jnp.int32)
    mine = raw_slots[...]
    tiled = jnp.concatenate([mine, mine, mine, mine], axis=1)
    is_valid = lanes(tiled.shape) % CAP < count_column
    sent_slots[...] = jnp.where(is_valid, tiled, -1).reshape(MEMBERS, 1, BLOCK)
    row_slots[0] = sent_slots[me]

    sums[...] = jnp.zeros_like(sums)
    tally[...] = jnp.zeros_like(tally)

    load_values.wait()
    pl.semaphore_wait(barrier, MEMBERS - 1 + 2)

    def remote(source, target, send, recv, where):
        return pltpu.make_async_remote_copy(
            src_ref=source, dst_ref=target, send_sem=send, recv_sem=recv, device_id=where, device_id_type=MESH
        )

    here = {"grp": up, "mem": me}

    def send_slots(k, _):
        to = member_at(me, k // PER_CHUNK, k % PER_CHUNK, 1)
        remote(
            sent_slots.at[to], row_slots.at[k], send_sem.at[0], slot_sem.at[0], {"grp": group, "mem": to}
        ).start()
        return 0

    def send_values(k, _):
        chunk, place = k // PER_CHUNK, k % PER_CHUNK
        to = member_at(me, chunk, place, 1)
        remote(
            vals.at[to], rows.at[chunk, place], send_sem.at[1], own_sem.at[chunk], {"grp": group, "mem": to}
        ).start()
        return 0

    lax.fori_loop(1, MEMBERS, send_slots, 0)
    lax.fori_loop(1, MEMBERS, send_values, 0)

    def landed(ref, sem):
        remote(ref, ref, send_sem.at[0], sem, here).wait_recv()

    def left(ref, sem):
        remote(ref, ref, sem, ring_sem.at[0], here).wait_send()

    def spread_slots(source):
        first = source * MEMBERS
        got = row_slots[pl.ds(first, MEMBERS)].reshape(MEMBERS, BLOCK)
        turn = lax.broadcasted_iota(jnp.int32, got.shape, 0) % 4
        flat[...] = jnp.where(lanes(got.shape) // CAP == turn, got, 0)
        quarter = MEMBERS // 4
        joined = flat[pl.ds(0, quarter, stride=4), :]
        for i in range(1, 4):
            joined = joined + flat[pl.ds(i, quarter, stride=4), :]
        lane_slots[pl.ds(pl.multiple_of(source * quarter, quarter), quarter), :] = joined
        turned = jnp.transpose(got)
        for k in range(MEMBERS):
            wide_slots[first + k] = jnp.broadcast_to(turned[:CAP, k : k + 1], (CAP, BLOCK))

    own_rows = row_slots.at[pl.ds(0, MEMBERS)]
    landed(row_slots.at[pl.ds(1, MEMBERS - 1)], slot_sem.at[0])
    remote(
        own_rows, row_slots.at[pl.ds(MEMBERS, MEMBERS)], send_sem.at[2], slot_sem.at[1], {"grp": up, "mem": me}
    ).start()
    remote(
        own_rows, row_slots.at[pl.ds(2 * MEMBERS, MEMBERS)], send_sem.at[2], slot_sem.at[2], {"grp": down, "mem": me}
    ).start()
    spread_slots(0)

    def on_own(chunk):
        @pl.when(chunk == 0)
        def _():
            load_own.wait()
            landed(rows.at[0, pl.ds(1, PER_CHUNK - 1)], own_sem.at[0])

        @pl.when(chunk > 0)
        def _():
            landed(rows.at[chunk], own_sem.at[chunk])

        remote(
            rows.at[chunk], rows.at[CHUNKS + chunk], send_sem.at[3], ring_sem.at[chunk], {"grp": up, "mem": me}
        ).start()
        remote(
            rows.at[chunk], rows.at[2 * CHUNKS + chunk], send_sem.at[3], ring_sem.at[CHUNKS + chunk],
            {"grp": down, "mem": me},
        ).start()

    some = PER_CHUNK // 2

    def on_below(chunk):
        landed(rows.at[CHUNKS + chunk], ring_sem.at[chunk])
        first = pl.ds(0, some)
        remote(
            rows.at[CHUNKS + chunk, first], rows.at[3 * CHUNKS + chunk, first], send_sem.at[4],
            ring_sem.at[2 * CHUNKS + chunk], {"grp": up, "mem": me},
        ).start()

    def on_above(chunk):
        landed(rows.at[2 * CHUNKS + chunk], ring_sem.at[CHUNKS + chunk])
        last = pl.ds(some, some)
        remote(
            rows.at[2 * CHUNKS + chunk, last], rows.at[3 * CHUNKS + chunk, last], send_sem.at[4],
            ring_sem.at[2 * CHUNKS + chunk], {"grp": down, "mem": me},
        ).start()

    def on_across(chunk):
        landed(rows.at[3 * CHUNKS + chunk], ring_sem.at[2 * CHUNKS + chunk])

    def add_piece(source, pair):
        at = source * MEMBERS + pair * PAIR
        wide = wide_slots[pl.ds(at, PAIR)].reshape(PIECE, BLOCK)
        got = rows[pl.ds(source * CHUNKS + 2 * pair, 2)].reshape(PIECE, BLOCK).astype(jnp.float32)
        second = jnp.where(wide >= HALF, got, 0.0)
        right = jnp.concatenate([got - second, second], axis=1).astype(jnp.bfloat16)
        four = lane_slots[pl.ds(source * (MEMBERS // 4) + pair * 4, 4), :]
        line = jnp.concatenate([four[i : i + 1] for i in range(4)], axis=1)
        place = lax.broadcasted_iota(jnp.int32, (HALF, PIECE), 0)
        chosen = jnp.where(place == in_half(line), 1.0, 0.0).astype(jnp.bfloat16)
        sums[...] += jnp.dot(chosen, right, preferred_element_type=jnp.float32)
        upper = lax.broadcasted_iota(jnp.int32, (MEMBERS, PIECE), 0)
        by_block = jnp.where(upper == line // BLOCK - (line < 0).astype(jnp.int32), 1.0, 0.0).astype(jnp.bfloat16)
        by_lane = jnp.where(lanes(wide.shape) == wide % BLOCK, 1.0, 0.0).astype(jnp.bfloat16)
        tally[...] += jnp.dot(by_block, by_lane, preferred_element_type=jnp.float32)

    def turn(step, _):
        source = step % GROUPS
        pair = step // GROUPS - (source + 1) // 2

        @pl.when((pair >= 0) & (pair < PIECES))
        def _():
            @pl.when((source == 1) & (pair == 0))
            def _():
                landed(row_slots.at[pl.ds(MEMBERS, MEMBERS)], slot_sem.at[1])
                landed(row_slots.at[pl.ds(2 * MEMBERS, MEMBERS)], slot_sem.at[2])
                half = MEMBERS // 2
                remote(
                    row_slots.at[pl.ds(MEMBERS, half)], row_slots.at[pl.ds(3 * MEMBERS, half)], send_sem.at[5],
                    slot_sem.at[3], {"grp": up, "mem": me},
                ).start()
                remote(
                    row_slots.at[pl.ds(2 * MEMBERS + half, half)], row_slots.at[pl.ds(3 * MEMBERS + half, half)],
                    send_sem.at[5], slot_sem.at[3], {"grp": down, "mem": me},
                ).start()

            @pl.when((source == 3) & (pair == 0))
            def _():
                landed(row_slots.at[pl.ds(3 * MEMBERS, MEMBERS)], slot_sem.at[3])

            @pl.when((source > 0) & (pair == 0))
            def _():
                spread_slots(source)

            for i in range(2):
                chunk = 2 * pair + i
                pl.when(source == 0)(functools.partial(on_own, chunk))
                pl.when(source == 1)(functools.partial(on_below, chunk))
                pl.when(source == 2)(functools.partial(on_above, chunk))
                pl.when(source == 3)(functools.partial(on_across, chunk))

            add_piece(source, pair)

        return 0

    lax.fori_loop(0, GROUPS * (PIECES + 2), turn, 0)

    scale = jnp.transpose(1.0 / jnp.maximum(tally[...], 1.0))
    for j in range(BUCKET // BLOCK):
        half, at = divmod(j * BLOCK, HALF)
        part = sums[at : at + BLOCK, half * BLOCK : (half + 1) * BLOCK]
        part = part * jnp.broadcast_to(scale[:, j : j + 1], (BLOCK, BLOCK))
        averaged[j * BLOCK : (j + 1) * BLOCK, :] = part
        mean[at : at + BLOCK, half * BLOCK : (half + 1) * BLOCK] = part.astype(jnp.bfloat16)
    store_averaged = pltpu.make_async_copy(averaged, averaged_out, out_sem.at[0])
    store_averaged.start()

    store_own = pltpu.make_async_copy(back.at[0, 0], returned_out.at[0, me], out_sem.at[1])

    def give_back(step, _):
        chunk = CHUNKS - 1 - step
        wide = wide_slots[pl.ds(chunk * PER_CHUNK, PER_CHUNK)].reshape(PER_CHUNK * CAP, BLOCK)
        offset = in_half(wide) - lanes(wide.shape)
        chosen = jnp.concatenate(
            [jnp.where(offset == i * BLOCK, 1.0, 0.0).astype(jnp.bfloat16) for i in range(HALF // BLOCK)], axis=1
        )
        both = jnp.dot(chosen, mean[...], preferred_element_type=jnp.float32)
        picked = jnp.where(wide >= HALF, both[:, BLOCK:], both[:, :BLOCK])
        picked = jnp.where(wide >= 0, picked, 0.0)
        back[chunk] = picked.astype(jnp.bfloat16).reshape(PER_CHUNK, CAP, BLOCK)

        def send_back(place, _):
            to = member_at(me, chunk, place, -1)
            remote(
                back.at[chunk, place], returned_out.at[0, me], send_sem.at[6], back_sem, {"grp": group, "mem": to}
            ).start()
            return 0

        @pl.when(chunk > 0)
        def _():
            lax.fori_loop(0, PER_CHUNK, send_back, 0)

        @pl.when(chunk == 0)
        def _():
            lax.fori_loop(1, PER_CHUNK, send_back, 0)
            store_own.start()

        return 0

    lax.fori_loop(0, CHUNKS, give_back, 0)

    left(sent_slots.at[pl.ds(0, MEMBERS - 1)], send_sem.at[0])
    left(vals.at[pl.ds(0, MEMBERS - 1)], send_sem.at[1])
    left(row_slots.at[pl.ds(0, 2 * MEMBERS)], send_sem.at[2])
    left(rows.at[pl.ds(0, 2 * CHUNKS)], send_sem.at[3])
    left(rows.at[pl.ds(0, CHUNKS)], send_sem.at[4])
    left(row_slots.at[pl.ds(0, MEMBERS)], send_sem.at[5])
    left(vals.at[pl.ds(0, MEMBERS - 1)], send_sem.at[6])
    store_own.wait()
    store_averaged.wait()
    landed(returned_out.at[0, pl.ds(0, MEMBERS - 1)], back_sem)


def per_device(values, slots, counts):
    anywhere = pl.BlockSpec(memory_space=pl.ANY)
    return pl.pallas_call(
        kernel,
        out_shape=(
            jax.ShapeDtypeStruct((BUCKET, BLOCK), jnp.float32),
            jax.ShapeDtypeStruct((1, MEMBERS, CAP, BLOCK), jnp.bfloat16),
        ),
        in_specs=[anywhere] * 3,
        out_specs=(anywhere, anywhere),
        scratch_shapes=[
            pltpu.VMEM((MEMBERS, CAP, BLOCK), jnp.bfloat16),
            pltpu.VMEM((MEMBERS, CAP), jnp.int32),
            pltpu.VMEM((1, MEMBERS), jnp.int32),
            pltpu.VMEM((MEMBERS, 1, BLOCK), jnp.int32),
            pltpu.VMEM((GROUPS * CHUNKS, PER_CHUNK, CAP, BLOCK), jnp.bfloat16),
            pltpu.VMEM((GROUPS * MEMBERS, 1, BLOCK), jnp.int32),
            pltpu.VMEM((MEMBERS, BLOCK), jnp.int32),
            pltpu.VMEM((GROUPS * MEMBERS // 4, BLOCK), jnp.int32),
            pltpu.VMEM((GROUPS * MEMBERS, CAP, BLOCK), jnp.int32),
            pltpu.VMEM((HALF, 2 * BLOCK), jnp.float32),
            pltpu.VMEM((MEMBERS, BLOCK), jnp.float32),
            pltpu.VMEM((HALF, 2 * BLOCK), jnp.bfloat16),
            pltpu.VMEM((BUCKET, BLOCK), jnp.float32),
            pltpu.VMEM((CHUNKS, PER_CHUNK, CAP, BLOCK), jnp.bfloat16),
            pltpu.SemaphoreType.DMA((4,)),
            pltpu.SemaphoreType.DMA((2,)),
            pltpu.SemaphoreType.DMA((7,)),
            pltpu.SemaphoreType.DMA((CHUNKS,)),
            pltpu.SemaphoreType.DMA((3 * CHUNKS,)),
            pltpu.SemaphoreType.DMA((4,)),
            pltpu.SemaphoreType.DMA,
        ],
        compiler_params=pltpu.CompilerParams(
            collective_id=0, has_side_effects=True, vmem_limit_bytes=60 * 2**20
        ),
        name="merge",
    )(values, slots, counts)


def solution(mesh):
    return jax.shard_map(
        per_device,
        mesh=mesh,
        in_specs=(
            P(("grp", "mem"), None, None, None),
            P(("grp", "mem"), None, None),
            P(("grp", "mem"), None),
        ),
        out_specs=(P("mem", None), P(("grp", "mem"), None, None, None)),
        check_vma=False,
    )
```

time: 191 us -> 72.7 us (0.38)
  waiting for transfers between devices: 75.8 us -> 0 us
  Pallas kernels: 0 us -> 65.5 us
  starting transfers between devices: 30.2 us -> 0 us
  other arithmetic: 27.1 us -> 0 us
  blocking collectives: 25.6 us -> 0 us
  matrix products: 14.8 us -> 0 us
  local copies, waits for them, and re-layouts: 15 us -> 6.38 us
    all_to_all x5 -> x0, waiting for transfers between devices: 75.8 us -> none  [the longest x2 42.5 us: summed_on_arrival(): pieces = lax.all_to_all(split_up(shard, dim, peers), axis, 0, 0, tiled=True)]
    pallas_call x0 -> x1, Pallas kernels: none -> 65.5 us  [per_device(): pl.pallas_call(kernel, out_shape=(jax.ShapeDtypeStruct((BUCKET, BLOCK), j...]
    all_to_all x5 -> x0, starting transfers between devices: 30.2 us -> none  [the longest x1 13 us: per_device(): lax.all_to_all(send_slots, 'mem', split_axis=0, concat_axis=0, tiled=True)]
    all_to_all x1 -> x0, blocking collectives: 25.6 us -> none  [per_device(): lax.all_to_all(back_rows, 'mem', split_axis=0, concat_axis=0, tiled=True)]
    dot_general x7 -> x0, matrix products: 14.8 us -> none  [one_tile(): return jnp.dot(onehot, rows_in, preferred_element_type=jnp.float32)]
    scatter-add x1 -> x0, other arithmetic: 12.4 us -> none  [live_counts(): jax.ops.segment_sum(live_in, jnp.maximum(slot_in, 0), num_segments=BUCKET)]
    gather x1 -> x0, local copies, waits for them, and re-layouts: 7.62 us -> none  [per_device(): owned_rows = jnp.take(averaged, jnp.maximum(slot_in, 0), axis=0)]
    unnamed x6 -> x5, local copies, waits for them, and re-layouts: 1.6 us -> 6.38 us
  transfers between devices with their start and end apart: 5 -> 0, of which waited for: 4 -> 0; matrix products, arithmetic and copies ran while one was open for 21% -> 0% of each run, Pallas kernels for 0% -> 0%
where the time goes in v1:
time: 72.7 us; the launch traced here: 72.6 us
  Pallas kernels  65.5 us (90%)
  local copies, waits for them, and re-layouts  6.38 us (9%)
    pallas_call x1, Pallas kernels, per_device(): pl.pallas_call(kernel, out_shape=(jax.ShapeDtypeStruct((BUCKET, BLOCK), j...  65.5 us
    unnamed x5, local copies, waits for them, and re-layouts  6.38 us

profile of v1, /device:TPU:1, one launch (start us, length us, event | category | flops | bytes accessed | tf_op | source)
XLA Modules:
  0.0 72.6 jit_solution(784692750481647916)
XLA Ops:
  0.6 1.4 %copy.5.slots = s32[1,64,32]{2,1,0:T(8,128)} copy(s32[1,64,32]{1,2,0:T(8,128)} %param.4) | data formatting | bytes 16384 | tf_op args[1]
  2.0 65.5 %merge.1 = (f32[7168,128]{1,0:T(8,128)}, bf16[1,64,32,128]{3,2,1,0:T(8,128)(2,1)}) custom-call(bf16[1,64,32,128]{3,2,1,0:T(8,128)(2,1)} %values.1, s32[1,64,32]{2,1,0:T(8,128)} %copy.5.slots, s32[1,64]{1,0:T(1,128)} %counts.1), custom_call_target="tpu_custom_call" | custom-call | tf_op jit(solution)/shard_map/merge/pallas_call | solution.py:304
  67.6 0.0 copy-start
  67.6 4.2 %copy.8 = f32[7168,128]{1,0:T(8,128)} copy(f32[7168,128]{1,0:T(8,128)} %get-tuple-element.4) | data formatting | bytes 7340032
  71.8 0.0 copy-done
  71.8 0.8 %copy.9 = bf16[1,64,32,128]{3,2,1,0:T(8,128)(2,1)} copy(bf16[1,64,32,128]{3,2,1,0:T(8,128)(2,1)S(1)} %copy-done) | data formatting | bytes 1048576
Async XLA Ops:
  67.6 4.2 %copy-start = (bf16[1,64,32,128]{3,2,1,0:T(8,128)(2,1)S(1)}, bf16[1,64,32,128]{3,2,1,0:T(8,128)(2,1)}, u32[]{:S(2)}) copy-start(bf16[1,64,32,128]{3,2,1,0:T(8,128)(2,1)} %get-tuple-element.5) | copy-start | bytes 1572868

commit v2 on v0

v2 whole, which is shorter than its diff:
```python
import functools

import jax
import jax.numpy as jnp
from jax import lax
from jax.experimental import pallas as pl
from jax.experimental.pallas import tpu as pltpu
from jax.sharding import PartitionSpec as P

MESH = pl.DeviceIdType.MESH

GROUPS = 4
MEMBERS = 64
CAP = 32
BLOCK = 128
BUCKET = 7168
HALF = BUCKET // 2
PER_CHUNK = 8
CHUNKS = MEMBERS // PER_CHUNK
ROWS = PER_CHUNK * CAP
EARLY = 2 * PER_CHUNK

OWN, BELOW, ABOVE, ACROSS = 0, CHUNKS, 2 * CHUNKS, 3 * CHUNKS

BELOW_SLOTS, ABOVE_SLOTS, ACROSS_SLOTS = 0, 2, 4


def z_step(chunk):
    odd = lax.rem(chunk, 2)
    return odd * lax.div(chunk + 1, 2) + (1 - odd) * lax.rem(8 - lax.div(chunk, 2), 8)


def lanes(shape):
    return lax.broadcasted_iota(jnp.int32, shape, len(shape) - 1)


def in_half(slot):
    return jnp.where(slot >= HALF, slot - HALF, slot)


def kernel(
    values_in, slots_in, counts_in, averaged_out, returned_out,
    values, slots, counts, sent_slots, rows, row_slots, wide_slots, sums, tally, mean, back,
    load_sem, send_sem, own_sem, ring_sem, own_slot_sem, slot_sem, back_sem,
):
    group = lax.axis_index("grp")
    me = lax.axis_index("mem")
    above = {"grp": lax.rem(group + 1, GROUPS), "mem": me}
    below = {"grp": lax.rem(group + GROUPS - 1, GROUPS), "mem": me}
    z, x, core = lax.div(me, 8), lax.rem(lax.div(me, 2), 4), lax.rem(me, 2)
    def columns(sign):
        cores = [lax.rem(core + i, 2) for i in range(2)]
        return [2 * lax.rem(x + 4 + sign * i, 4) + cores[j] for i in range(4) for j in range(2)]

    def everyone(chunk, sign, reach):
        z_to = 8 * lax.rem(z + 8 + sign * z_step(chunk), 8)
        for place, column in enumerate(columns(sign)):
            if place:
                reach(chunk, place, z_to + column)
            else:
                pl.when(chunk > 0)(functools.partial(reach, chunk, place, z_to + column))

    def remote(source, target, send, recv, where):
        return pltpu.make_async_remote_copy(
            src_ref=source, dst_ref=target, send_sem=send, recv_sem=recv, device_id=where, device_id_type=MESH
        )

    def landed(ref, sem):
        remote(ref, ref, send_sem.at[0], sem, above).wait_recv()

    def left(ref, sem):
        remote(ref, ref, sem, back_sem, above).wait_send()

    barrier = pltpu.get_barrier_semaphore()

    def greet(chunk, place, to):
        pl.semaphore_signal(barrier, inc=1, device_id={"grp": group, "mem": to}, device_id_type=MESH)

    with jax.named_scope("greet"):
        lax.fori_loop(0, CHUNKS, lambda i, _: everyone(CHUNKS - 1 - i, 1, greet) or 0, 0)
        for other in (above, below):
            pl.semaphore_signal(barrier, inc=1, device_id=other, device_id_type=MESH)

    loads = [
        pltpu.make_async_copy(source, target, load_sem.at[i])
        for i, (source, target) in enumerate(((slots_in, slots), (counts_in, counts), (values_in, values)))
    ]
    for load in loads:
        load.start()

    with jax.named_scope("prep"):
        for load in loads[:2]:
            load.wait()
        is_valid = lax.broadcasted_iota(jnp.int32, (CAP, MEMBERS), 0) < counts[...]
        masked = jnp.where(is_valid, slots[0], -1)
        tiled = jnp.transpose(jnp.concatenate([masked] * 4, axis=0))
        sent_slots[...] = tiled.reshape(MEMBERS, 1, BLOCK)
        row_slots[0] = sent_slots[me]
        loads[2].wait()
        rows[0, 0] = values[0, me]
        sums[...] = jnp.zeros_like(sums)
        tally[...] = jnp.zeros_like(tally)

    with jax.named_scope("barrier"):
        pl.semaphore_wait(barrier, MEMBERS - 1 + 2)

    def send_slots(chunk, place, to):
        remote(
            sent_slots.at[to], row_slots.at[chunk * PER_CHUNK + place], send_sem.at[0], own_slot_sem.at[chunk],
            {"grp": group, "mem": to},
        ).start()

    def send_values(chunk, place, to):
        remote(
            values.at[0, to], rows.at[chunk, place], send_sem.at[1], own_sem.at[chunk], {"grp": group, "mem": to}
        ).start()

    with jax.named_scope("sends"):
        lax.fori_loop(0, CHUNKS, lambda i, _: everyone(i, 1, send_slots) or 0, 0)
        lax.fori_loop(0, CHUNKS, lambda i, _: everyone(i, 1, send_values) or 0, 0)

    def slot_block(source, part, side=None):
        first, count = (EARLY, MEMBERS - EARLY) if part else (0, EARLY)
        if side is not None:
            count = count // 2
            first = first + side * count
        return row_slots.at[pl.ds(source * PER_CHUNK + first, count)]

    def on_own(chunk):
        if isinstance(chunk, int) and chunk == 0:
            landed(rows.at[0, pl.ds(1, PER_CHUNK - 1)], own_sem.at[0])
        else:
            landed(rows.at[chunk], own_sem.at[chunk])
        remote(rows.at[chunk], rows.at[BELOW + chunk], send_sem.at[3], ring_sem.at[chunk], above).start()
        remote(rows.at[chunk], rows.at[ABOVE + chunk], send_sem.at[3], ring_sem.at[CHUNKS + chunk], below).start()

    some = PER_CHUNK // 2

    def on_ring(chunk):
        landed(rows.at[BELOW + chunk], ring_sem.at[chunk])
        first, last = pl.ds(0, some), pl.ds(some, some)
        remote(
            rows.at[BELOW + chunk, first], rows.at[ACROSS + chunk, first], send_sem.at[4],
            ring_sem.at[2 * CHUNKS + chunk], above,
        ).start()
        landed(rows.at[ABOVE + chunk], ring_sem.at[CHUNKS + chunk])
        remote(
            rows.at[ABOVE + chunk, last], rows.at[ACROSS + chunk, last], send_sem.at[4],
            ring_sem.at[2 * CHUNKS + chunk], below,
        ).start()

    def on_across(chunk):
        landed(rows.at[ACROSS + chunk], ring_sem.at[2 * CHUNKS + chunk])

    def widen(chunk):
        first = chunk * PER_CHUNK
        turned = jnp.transpose(row_slots[pl.ds(first, PER_CHUNK)].reshape(PER_CHUNK, BLOCK))
        for k in range(PER_CHUNK):
            wide_slots[first + k] = jnp.broadcast_to(turned[:CAP, k : k + 1], (CAP, BLOCK))

    def wide_of(chunk):
        return wide_slots[pl.ds(chunk * PER_CHUNK, PER_CHUNK)].reshape(ROWS, BLOCK)

    def lines_of(chunk):
        got = row_slots[pl.ds(chunk * PER_CHUNK, PER_CHUNK)].reshape(PER_CHUNK, BLOCK)
        quarter = lanes((1, BLOCK)) // CAP
        lines = []
        for q in range(0, PER_CHUNK, 4):
            line = got[q : q + 1]
            for i in range(1, 4):
                line = jnp.where(quarter == i, got[q + i : q + i + 1], line)
            lines.append(line)
        return lines

    def add(chunks, later):
        line = jnp.concatenate([line for chunk in chunks for line in lines_of(chunk)], axis=1)
        wide = jnp.concatenate([wide_of(chunk) for chunk in chunks], axis=0)
        got = jnp.concatenate([rows[chunk].reshape(ROWS, BLOCK) for chunk in chunks], axis=0).astype(jnp.float32)
        second = jnp.where(wide >= HALF, got, 0.0)
        right = jnp.concatenate([got - second, second], axis=1).astype(jnp.bfloat16)
        place = lax.broadcasted_iota(jnp.int32, (HALF, line.shape[1]), 0)
        chosen = jnp.where(place == in_half(line), 1.0, 0.0).astype(jnp.bfloat16)
        sums[...] += jnp.dot(chosen, right, preferred_element_type=jnp.float32)
        over = line - lax.broadcasted_iota(jnp.int32, (MEMBERS, line.shape[1]), 0) * BLOCK
        by_block = jnp.where((over >= 0) & (over < BLOCK), 1.0, 0.0).astype(jnp.bfloat16)
        by_lane = jnp.where(lanes(wide.shape) == (wide & (BLOCK - 1)), 1.0, 0.0).astype(jnp.bfloat16)
        tally[...] += jnp.dot(by_block, by_lane, preferred_element_type=jnp.float32)
        for chunk in later:
            widen(chunk)

    def own_slots(chunk):
        first = 0 if chunk else 1
        landed(row_slots.at[pl.ds(chunk * PER_CHUNK + first, PER_CHUNK - first)], own_slot_sem.at[chunk])

    def pass_slots(part):
        for source, sem, to in ((BELOW, BELOW_SLOTS, above), (ABOVE, ABOVE_SLOTS, below)):
            remote(
                slot_block(OWN, part), slot_block(source, part), send_sem.at[2], slot_sem.at[sem + part], to
            ).start()

    def ring_slots(part):
        for side, (source, sem, to) in enumerate(((BELOW, BELOW_SLOTS, above), (ABOVE, ABOVE_SLOTS, below))):
            landed(slot_block(source, part), slot_sem.at[sem + part])
            remote(
                slot_block(source, part, side), slot_block(ACROSS, part, side), send_sem.at[5],
                slot_sem.at[ACROSS_SLOTS + part], to,
            ).start()

    def across_slots(part):
        landed(slot_block(ACROSS, part), slot_sem.at[ACROSS_SLOTS + part])

    def pair(source, index):
        return [source + 2 * index, source + 2 * index + 1]

    def around(index):
        return pair(BELOW, index) + pair(ABOVE, index)

    def both(action, index):
        action(2 * index)
        action(2 * index + 1)

    def early(step, _):
        @pl.when(step == 0)
        def _():
            with jax.named_scope("w0"):
                both(own_slots, 0)
                pass_slots(0)
                both(on_own, 0)
                widen(OWN)
                widen(OWN + 1)

        @pl.when(step == 1)
        def _():
            with jax.named_scope("w1"):
                for i in range(1, CHUNKS // 2):
                    both(own_slots, i)
                pass_slots(1)
                both(on_own, 1)
                widen(OWN + 2)
                widen(OWN + 3)

        @pl.when(step == 2)
        def _():
            with jax.named_scope("w2"):
                ring_slots(0)
                widen(BELOW)
                widen(ABOVE)
                on_ring(0)

        @pl.when(step == 3)
        def _():
            with jax.named_scope("w3"):
                on_ring(1)

        ring, odd = lax.div(step, 2), lax.rem(step, 2)
        first = (1 - ring) * 2 * odd + ring * (BELOW + odd)
        second = first + 1 + ring * (ABOVE - BELOW - 1)
        next_first = ring * ((1 - odd) * (BELOW + 1) + odd * (OWN + 4))
        next_second = 1 + ring * ((1 - odd) * ABOVE + odd * (OWN + 4))
        with jax.named_scope("early"):
            add([first, second], [next_first, next_second])
        return 0

    lax.fori_loop(0, 4, early, 0)

    last = CHUNKS // 2 - 1

    def late(step, _):
        @pl.when(step <= last)
        def _():
            @pl.when(step == 2)
            def _():
                with jax.named_scope("w_own"):
                    both(on_own, 2)
                    ring_slots(1)

            with jax.named_scope("own"):
                add(pair(OWN, step), around(step - 1) + pair(OWN, last))

        @pl.when(step <= last + 1)
        def _():
            with jax.named_scope("w_ring"):
                both(on_ring, step - 1)

                for part in range(2):
                    pl.when(step == 2 + part)(functools.partial(across_slots, part))

            with jax.named_scope("ring"):
                add(around(step - 1), pair(ACROSS, step - 2))

        @pl.when(step == 2)
        def _():
            with jax.named_scope("w_own3"):
                both(on_own, last)

        with jax.named_scope("w_across"):
            both(on_across, step - 2)
        with jax.named_scope("across"):
            after = jnp.where(step > 2, jnp.minimum(step - 1, last), 0)
            add(pair(ACROSS, step - 2), around(jnp.minimum(step, last)) + pair(ACROSS, after))
        return 0

    lax.fori_loop(2, last + 3, late, 0)

    with jax.named_scope("mean"):
        scale = jnp.transpose(1.0 / jnp.maximum(tally[...], 1.0))
        for j in range(BUCKET // BLOCK):
            side, at = divmod(j * BLOCK, HALF)
            part = sums[at : at + BLOCK, side * BLOCK : (side + 1) * BLOCK]
            part = part * jnp.broadcast_to(scale[:, j : j + 1], (BLOCK, BLOCK))
            averaged_out[j * BLOCK : (j + 1) * BLOCK, :] = part
            mean[at : at + BLOCK, side * BLOCK : (side + 1) * BLOCK] = part.astype(jnp.bfloat16)

    def give_back(step, _):
        chunk = CHUNKS - 1 - step
        with jax.named_scope("gather"):
            wide = wide_of(chunk)
            offset = in_half(wide) - lanes(wide.shape)
            chosen = jnp.concatenate(
                [jnp.where(offset == i * BLOCK, 1.0, 0.0).astype(jnp.bfloat16) for i in range(HALF // BLOCK)], axis=1
            )
            sides = jnp.dot(chosen, mean[...], preferred_element_type=jnp.float32)
            picked = jnp.where(wide >= HALF, sides[:, BLOCK:], sides[:, :BLOCK])
            picked = jnp.where(wide >= 0, picked, 0.0)
            back[chunk] = picked.astype(jnp.bfloat16).reshape(PER_CHUNK, CAP, BLOCK)

        def send_back(chunk, place, to):
            remote(
                back.at[chunk, place], returned_out.at[0, me], send_sem.at[6], back_sem, {"grp": group, "mem": to}
            ).start()

        with jax.named_scope("sendback"):
            everyone(chunk, -1, send_back)

        return 0

    lax.fori_loop(0, CHUNKS, give_back, 0)
    returned_out[0, me] = back[0, 0]

    most = pl.ds(0, MEMBERS - 1)
    with jax.named_scope("lefts"):
        left(sent_slots.at[most], send_sem.at[0])
        left(values.at[0, most], send_sem.at[1])
        left(row_slots.at[pl.ds(0, 2 * MEMBERS)], send_sem.at[2])
        left(rows.at[pl.ds(0, 2 * CHUNKS)], send_sem.at[3])
        left(rows.at[pl.ds(0, CHUNKS)], send_sem.at[4])
        left(row_slots.at[pl.ds(0, MEMBERS)], send_sem.at[5])
        left(values.at[0, most], send_sem.at[6])
    with jax.named_scope("waitback"):
        landed(returned_out.at[0, most], back_sem)


PARTS = 8


def hand_over(averaged, returned, averaged_out, returned_out, sem):
    part = BUCKET // PARTS
    copies = [pltpu.make_async_copy(returned, returned_out, sem.at[PARTS])]
    for i in range(PARTS):
        at = pl.ds(i * part, part)
        copies.append(pltpu.make_async_copy(averaged.at[at], averaged_out.at[at], sem.at[i]))
    for copy in copies:
        copy.start()
    for copy in copies:
        copy.wait()


def per_device(values, slots, counts):
    in_hbm = pl.BlockSpec(memory_space=pltpu.HBM)
    in_vmem = pl.BlockSpec(memory_space=pltpu.VMEM)
    operands = [pltpu.with_memory_space_constraint(x, pltpu.HBM) for x in (values, jnp.swapaxes(slots, 1, 2), counts)]
    results = pl.pallas_call(
        kernel,
        out_shape=(
            jax.ShapeDtypeStruct((BUCKET, BLOCK), jnp.float32),
            jax.ShapeDtypeStruct((1, MEMBERS, CAP, BLOCK), jnp.bfloat16),
        ),
        in_specs=[in_hbm] * 3,
        out_specs=(in_vmem, in_vmem),
        scratch_shapes=[
            pltpu.VMEM((1, MEMBERS, CAP, BLOCK), jnp.bfloat16),
            pltpu.VMEM((1, CAP, MEMBERS), jnp.int32),
            pltpu.VMEM((1, MEMBERS), jnp.int32),
            pltpu.VMEM((MEMBERS, 1, BLOCK), jnp.int32),
            pltpu.VMEM((GROUPS * CHUNKS, PER_CHUNK, CAP, BLOCK), jnp.bfloat16),
            pltpu.VMEM((GROUPS * MEMBERS, 1, BLOCK), jnp.int32),
            pltpu.VMEM((GROUPS * MEMBERS, CAP, BLOCK), jnp.int32),
            pltpu.VMEM((HALF, 2 * BLOCK), jnp.float32),
            pltpu.VMEM((MEMBERS, BLOCK), jnp.float32),
            pltpu.VMEM((HALF, 2 * BLOCK), jnp.bfloat16),
            pltpu.VMEM((CHUNKS, PER_CHUNK, CAP, BLOCK), jnp.bfloat16),
            pltpu.SemaphoreType.DMA((3,)),
            pltpu.SemaphoreType.DMA((7,)),
            pltpu.SemaphoreType.DMA((CHUNKS,)),
            pltpu.SemaphoreType.DMA((3 * CHUNKS,)),
            pltpu.SemaphoreType.DMA((CHUNKS,)),
            pltpu.SemaphoreType.DMA((6,)),
            pltpu.SemaphoreType.DMA,
        ],
        compiler_params=pltpu.CompilerParams(
            collective_id=0, has_side_effects=True, vmem_limit_bytes=40 * 2**20
        ),
        name="merge",
    )(*operands)
    return pl.pallas_call(
        hand_over,
        out_shape=[jax.ShapeDtypeStruct(x.shape, x.dtype) for x in results],
        in_specs=[in_vmem, in_vmem],
        out_specs=[in_hbm, in_hbm],
        scratch_shapes=[pltpu.SemaphoreType.DMA((PARTS + 1,))],
        compiler_params=pltpu.CompilerParams(vmem_limit_bytes=2**20),
        name="hand_over",
    )(*results)


def solution(mesh):
    return jax.shard_map(
        per_device,
        mesh=mesh,
        in_specs=(
            P(("grp", "mem"), None, None, None),
            P(("grp", "mem"), None, None),
            P(("grp", "mem"), None),
        ),
        out_specs=(P("mem", None), P(("grp", "mem"), None, None, None)),
        check_vma=False,
    )
```

time: 191 us -> 60.9 us (0.32)
  waiting for transfers between devices: 75.8 us -> 0 us
  Pallas kernels: 0 us -> 60.1 us
  starting transfers between devices: 30.2 us -> 0 us
  other arithmetic: 27.1 us -> 0 us
  blocking collectives: 25.6 us -> 0 us
  local copies, waits for them, and re-layouts: 15 us -> 0 us
  matrix products: 14.8 us -> 0 us
    all_to_all x5 -> x0, waiting for transfers between devices: 75.8 us -> none  [the longest x2 42.5 us: summed_on_arrival(): pieces = lax.all_to_all(split_up(shard, dim, peers), axis, 0, 0, tiled=True)]
    pallas_call x0 -> x2, Pallas kernels: none -> 60.1 us  [the longest x1 58 us: per_device(): pl.pallas_call(kernel, out_shape=(jax.ShapeDtypeStruct((BUCKET, BLOCK), j...]
    all_to_all x5 -> x0, starting transfers between devices: 30.2 us -> none  [the longest x1 13 us: per_device(): lax.all_to_all(send_slots, 'mem', split_axis=0, concat_axis=0, tiled=True)]
    all_to_all x1 -> x0, blocking collectives: 25.6 us -> none  [per_device(): lax.all_to_all(back_rows, 'mem', split_axis=0, concat_axis=0, tiled=True)]
    dot_general x7 -> x0, matrix products: 14.8 us -> none  [one_tile(): return jnp.dot(onehot, rows_in, preferred_element_type=jnp.float32)]
    scatter-add x1 -> x0, other arithmetic: 12.4 us -> none  [live_counts(): jax.ops.segment_sum(live_in, jnp.maximum(slot_in, 0), num_segments=BUCKET)]
    gather x1 -> x0, local copies, waits for them, and re-layouts: 7.62 us -> none  [per_device(): owned_rows = jnp.take(averaged, jnp.maximum(slot_in, 0), axis=0)]
    add x7 -> x0, other arithmetic: 4.53 us -> none  [one_tile(): wanted = first + lax.broadcasted_iota(jnp.int32, (tile, 1), 0)]
  transfers between devices with their start and end apart: 5 -> 0, of which waited for: 4 -> 0; matrix products, arithmetic and copies ran while one was open for 21% -> 0% of each run, Pallas kernels for 0% -> 0%
where the time goes in v2:
time: 60.9 us; the launch traced here: 60.7 us
  Pallas kernels  60.1 us (99%)
  between operations  0.64 us (1%)
    pallas_call x1, Pallas kernels, per_device(): pl.pallas_call(kernel, out_shape=(jax.ShapeDtypeStruct((BUCKET, BLOCK), j...  58 us
    pallas_call x1, Pallas kernels, per_device(): pl.pallas_call(hand_over, out_shape=[jax.ShapeDtypeStruct(x.shape, x.dtyp...  2.08 us

profile of v2, /device:TPU:1, one launch (start us, length us, event | category | flops | bytes accessed | tf_op | source)
XLA Modules:
  0.0 60.7 jit_solution(17080744193401737482)
XLA Ops:
  0.6 58.0 %merge.1 = (f32[7168,128]{1,0:T(8,128)S(1)}, bf16[1,64,32,128]{3,2,1,0:T(8,128)(2,1)S(1)}) custom-call(bf16[1,64,32,128]{3,2,1,0:T(8,128)(2,1)} %values_in.1, s32[1,32,64]{2,1,0:T(8,128)} %bitcast.1, s32[1,64]{1,0:T(1,128)} %counts_in.1), custom_call_target="tpu_custom_call" | custom-call | tf_op jit(solution)/shard_map/merge/pallas_call | solution.py:372
  58.6 2.1 %hand_over.1 = (f32[7168,128]{1,0:T(8,128)}, bf16[1,64,32,128]{3,2,1,0:T(8,128)(2,1)}) custom-call(f32[7168,128]{1,0:T(8,128)S(1)} %get-tuple-element.4.averaged, bf16[1,64,32,128]{3,2,1,0:T(8,128)(2,1)S(1)} %get-tuple-element.5.returned), custom_call_target="tpu_custom_call" | custom-call | tf_op jit(solution)/shard_map/hand_over/pallas_call | solution.py:405

commit v3 on v2

--- a/solution.py
+++ b/solution.py
@@ -175,18 +175,29 @@
     def add(chunks, later):
         line = jnp.concatenate([line for chunk in chunks for line in lines_of(chunk)], axis=1)
         wide = jnp.concatenate([wide_of(chunk) for chunk in chunks], axis=0)
+        over = line - lax.broadcasted_iota(jnp.int32, (MEMBERS, line.shape[1]), 0) * BLOCK
+        by_block = jnp.where((over >= 0) & (over < BLOCK), 1.0, 0.0).astype(jnp.bfloat16)
+        by_lane = jnp.where(lanes(wide.shape) == (wide & (BLOCK - 1)), 1.0, 0.0).astype(jnp.bfloat16)
+        tally[...] += jnp.dot(by_block, by_lane, preferred_element_type=jnp.float32)
         got = jnp.concatenate([rows[chunk].reshape(ROWS, BLOCK) for chunk in chunks], axis=0).astype(jnp.float32)
         second = jnp.where(wide >= HALF, got, 0.0)
         right = jnp.concatenate([got - second, second], axis=1).astype(jnp.bfloat16)
         place = lax.broadcasted_iota(jnp.int32, (HALF, line.shape[1]), 0)
         chosen = jnp.where(place == in_half(line), 1.0, 0.0).astype(jnp.bfloat16)
         sums[...] += jnp.dot(chosen, right, preferred_element_type=jnp.float32)
-        over = line - lax.broadcasted_iota(jnp.int32, (MEMBERS, line.shape[1]), 0) * BLOCK
-        by_block = jnp.where((over >= 0) & (over < BLOCK), 1.0, 0.0).astype(jnp.bfloat16)
-        by_lane = jnp.where(lanes(wide.shape) == (wide & (BLOCK - 1)), 1.0, 0.0).astype(jnp.bfloat16)
-        tally[...] += jnp.dot(by_block, by_lane, preferred_element_type=jnp.float32)
         for chunk in later:
             widen(chunk)
+
+    def finish():
+        scale = jnp.transpose(1.0 / jnp.maximum(tally[...], 1.0))
+        for j in range(HALF // BLOCK):
+            at = j * BLOCK
+            for side in range(2):
+                column = side * (HALF // BLOCK) + j
+                part = sums[at : at + BLOCK, side * BLOCK : (side + 1) * BLOCK]
+                part = part * jnp.broadcast_to(scale[:, column : column + 1], (BLOCK, BLOCK))
+                averaged_out[side * HALF + at : side * HALF + at + BLOCK, :] = part
+                mean[at : at + BLOCK, side * BLOCK : (side + 1) * BLOCK] = part.astype(jnp.bfloat16)
 
     def own_slots(chunk):
         first = 0 if chunk else 1
@@ -219,6 +230,12 @@
         action(2 * index)
         action(2 * index + 1)
 
+    def pick(step, *values):
+        at = values[0]
+        for k in range(1, len(values)):
+            at = jnp.where(step == k, values[k], at)
+        return at
+
     def early(step, _):
         @pl.when(step == 0)
         def _():
@@ -251,65 +268,66 @@
         def _():
             with jax.named_scope("w3"):
                 on_ring(1)
-
-        ring, odd = lax.div(step, 2), lax.rem(step, 2)
-        first = (1 - ring) * 2 * odd + ring * (BELOW + odd)
-        second = first + 1 + ring * (ABOVE - BELOW - 1)
-        next_first = ring * ((1 - odd) * (BELOW + 1) + odd * (OWN + 4))
-        next_second = 1 + ring * ((1 - odd) * ABOVE + odd * (OWN + 4))
+                ring_slots(1)
+
+        chunks = zip(pair(OWN, 0), pair(OWN, 1), (BELOW, ABOVE), (BELOW + 1, ABOVE + 1))
+        later = zip(pair(OWN, 0) * 2, pair(OWN, 0) * 2, (BELOW + 1, ABOVE + 1) * 2, around(1))
         with jax.named_scope("early"):
-            add([first, second], [next_first, next_second])
+            add([pick(step, *options) for options in chunks], [pick(step, *options) for options in later])
         return 0
 
     lax.fori_loop(0, 4, early, 0)
 
     last = CHUNKS // 2 - 1
+    none = [0] * 4
 
     def late(step, _):
-        @pl.when(step <= last)
-        def _():
-            @pl.when(step == 2)
+        @pl.when((step == 0) | (step == 3) | (step == 4))
+        def _():
+            @pl.when(step == 0)
             def _():
-                with jax.named_scope("w_own"):
-                    both(on_own, 2)
-                    ring_slots(1)
-
-            with jax.named_scope("own"):
-                add(pair(OWN, step), around(step - 1) + pair(OWN, last))
-
-        @pl.when(step <= last + 1)
-        def _():
-            with jax.named_scope("w_ring"):
-                both(on_ring, step - 1)
-
-                for part in range(2):
-                    pl.when(step == 2 + part)(functools.partial(across_slots, part))
-
+                with jax.named_scope("wr0"):
+                    on_own(4)
+                    both(on_ring, 1)
+
+            @pl.when(step > 0)
+            def _():
+                with jax.named_scope("wr"):
+                    both(on_ring, step - 1)
+                    pl.when(step == 3)(functools.partial(across_slots, 1))
+
+            chunks = zip(around(1), none, none, around(2), around(3))
+            later = zip(pair(OWN, 2) * 2, none, none, around(3), pair(ACROSS, 1) * 2)
             with jax.named_scope("ring"):
-                add(around(step - 1), pair(ACROSS, step - 2))
-
-        @pl.when(step == 2)
-        def _():
-            with jax.named_scope("w_own3"):
-                both(on_own, last)
-
-        with jax.named_scope("w_across"):
-            both(on_across, step - 2)
-        with jax.named_scope("across"):
-            after = jnp.where(step > 2, jnp.minimum(step - 1, last), 0)
-            add(pair(ACROSS, step - 2), around(jnp.minimum(step, last)) + pair(ACROSS, after))
+                add([pick(step, *options) for options in chunks], [pick(step, *options) for options in later])
+
+        @pl.when(step != 3)
+        def _():
+            @pl.when(step < 3)
+            def _():
+                with jax.named_scope("wo"):
+                    on_own(5 + step)
+                    pl.when(step == 0)(functools.partial(across_slots, 0))
+                    pl.when(step == 1)(functools.partial(both, on_across, 0))
+
+            @pl.when(step > 3)
+            def _():
+                with jax.named_scope("wa"):
+                    both(on_across, step - 3)
+
+            chunks = zip(pair(OWN, 2), pair(ACROSS, 0), pair(OWN, 3), (0, 0), pair(ACROSS, 1), pair(ACROSS, 2))
+            later = zip(pair(ACROSS, 0) * 2, pair(OWN, 3) * 2, around(2), none, pair(ACROSS, 2) * 2, pair(ACROSS, 3) * 2)
+            with jax.named_scope("single"):
+                add([pick(step, *options) for options in chunks], [pick(step, *options) for options in later])
+
         return 0
 
-    lax.fori_loop(2, last + 3, late, 0)
-
-    with jax.named_scope("mean"):
-        scale = jnp.transpose(1.0 / jnp.maximum(tally[...], 1.0))
-        for j in range(BUCKET // BLOCK):
-            side, at = divmod(j * BLOCK, HALF)
-            part = sums[at : at + BLOCK, side * BLOCK : (side + 1) * BLOCK]
-            part = part * jnp.broadcast_to(scale[:, j : j + 1], (BLOCK, BLOCK))
-            averaged_out[j * BLOCK : (j + 1) * BLOCK, :] = part
-            mean[at : at + BLOCK, side * BLOCK : (side + 1) * BLOCK] = part.astype(jnp.bfloat16)
+    lax.fori_loop(0, 6, late, 0)
+    with jax.named_scope("w_last"):
+        both(on_across, last)
+    with jax.named_scope("last"):
+        add(pair(ACROSS, last), [])
+        finish()
 
     def give_back(step, _):
         chunk = CHUNKS - 1 - step

time: 60.9 us -> 59.8 us (0.982)
  Pallas kernels: 60.1 us -> 59 us
    pallas_call x1, Pallas kernels: 58 us -> 56.9 us  [per_device(): pl.pallas_call(kernel, out_shape=(jax.ShapeDtypeStruct((BUCKET, BLOCK), j...]
where the time goes in v3:
time: 59.8 us; the launch traced here: 59.6 us
  Pallas kernels  59 us (99%)
  between operations  0.64 us (1%)
    pallas_call x1, Pallas kernels, per_device(): pl.pallas_call(kernel, out_shape=(jax.ShapeDtypeStruct((BUCKET, BLOCK), j...  56.9 us
    pallas_call x1, Pallas kernels, per_device(): pl.pallas_call(hand_over, out_shape=[jax.ShapeDtypeStruct(x.shape, x.dtyp...  2.08 us

profile of v3, /device:TPU:1, one launch (start us, length us, event | category | flops | bytes accessed | tf_op | source)
XLA Modules:
  0.0 59.6 jit_solution(480458585194714448)
XLA Ops:
  0.6 56.9 %merge.1 = (f32[7168,128]{1,0:T(8,128)S(1)}, bf16[1,64,32,128]{3,2,1,0:T(8,128)(2,1)S(1)}) custom-call(bf16[1,64,32,128]{3,2,1,0:T(8,128)(2,1)} %values_in.1, s32[1,32,64]{2,1,0:T(8,128)} %bitcast.1, s32[1,64]{1,0:T(1,128)} %counts_in.1), custom_call_target="tpu_custom_call" | custom-call | tf_op jit(solution)/shard_map/merge/pallas_call | solution.py:390
  57.6 2.1 %hand_over.1 = (f32[7168,128]{1,0:T(8,128)}, bf16[1,64,32,128]{3,2,1,0:T(8,128)(2,1)}) custom-call(f32[7168,128]{1,0:T(8,128)S(1)} %get-tuple-element.4.averaged, bf16[1,64,32,128]{3,2,1,0:T(8,128)(2,1)S(1)} %get-tuple-element.5.returned), custom_call_target="tpu_custom_call" | custom-call | tf_op jit(solution)/shard_map/hand_over/pallas_call | solution.py:423

commit v4 on v3

--- a/solution.py
+++ b/solution.py
@@ -47,6 +47,7 @@
     me = lax.axis_index("mem")
     above = {"grp": lax.rem(group + 1, GROUPS), "mem": me}
     below = {"grp": lax.rem(group + GROUPS - 1, GROUPS), "mem": me}
+    across = {"grp": lax.rem(group + 2, GROUPS), "mem": me}
     z, x, core = lax.div(me, 8), lax.rem(lax.div(me, 2), 4), lax.rem(me, 2)
     def columns(sign):
         cores = [lax.rem(core + i, 2) for i in range(2)]
@@ -78,7 +79,7 @@
 
     with jax.named_scope("greet"):
         lax.fori_loop(0, CHUNKS, lambda i, _: everyone(CHUNKS - 1 - i, 1, greet) or 0, 0)
-        for other in (above, below):
+        for other in (above, below, across):
             pl.semaphore_signal(barrier, inc=1, device_id=other, device_id_type=MESH)
 
     loads = [
@@ -102,7 +103,7 @@
         tally[...] = jnp.zeros_like(tally)
 
     with jax.named_scope("barrier"):
-        pl.semaphore_wait(barrier, MEMBERS - 1 + 2)
+        pl.semaphore_wait(barrier, MEMBERS - 1 + GROUPS - 1)
 
     def send_slots(chunk, place, to):
         remote(
@@ -133,10 +134,18 @@
             landed(rows.at[chunk], own_sem.at[chunk])
         remote(rows.at[chunk], rows.at[BELOW + chunk], send_sem.at[3], ring_sem.at[chunk], above).start()
         remote(rows.at[chunk], rows.at[ABOVE + chunk], send_sem.at[3], ring_sem.at[CHUNKS + chunk], below).start()
+        if isinstance(chunk, int) and chunk == CHUNKS - 1:
+            remote(
+                rows.at[chunk], rows.at[ACROSS + chunk], send_sem.at[3], ring_sem.at[2 * CHUNKS + chunk], across
+            ).start()
 
     some = PER_CHUNK // 2
 
     def on_ring(chunk):
+        if isinstance(chunk, int) and chunk == CHUNKS - 1:
+            landed(rows.at[BELOW + chunk], ring_sem.at[chunk])
+            landed(rows.at[ABOVE + chunk], ring_sem.at[CHUNKS + chunk])
+            return
         landed(rows.at[BELOW + chunk], ring_sem.at[chunk])
         first, last = pl.ds(0, some), pl.ds(some, some)
         remote(
@@ -259,6 +268,7 @@
         @pl.when(step == 2)
         def _():
             with jax.named_scope("w2"):
+                on_own(4)
                 ring_slots(0)
                 widen(BELOW)
                 widen(ABOVE)
@@ -270,59 +280,72 @@
                 on_ring(1)
                 ring_slots(1)
 
-        chunks = zip(pair(OWN, 0), pair(OWN, 1), (BELOW, ABOVE), (BELOW + 1, ABOVE + 1))
-        later = zip(pair(OWN, 0) * 2, pair(OWN, 0) * 2, (BELOW + 1, ABOVE + 1) * 2, around(1))
+        @pl.when(step == 4)
+        def _():
+            with jax.named_scope("w4"):
+                on_ring(2)
+
+        chunks = zip(pair(OWN, 0), pair(OWN, 1), (BELOW, ABOVE), (BELOW + 1, ABOVE + 1), (OWN + 4, BELOW + 2))
+        later = zip(pair(OWN, 0) * 2, pair(OWN, 0) * 2, (BELOW + 1, ABOVE + 1) * 2, (OWN + 4, BELOW + 2) * 2, mixed)
         with jax.named_scope("early"):
             add([pick(step, *options) for options in chunks], [pick(step, *options) for options in later])
         return 0
 
-    lax.fori_loop(0, 4, early, 0)
+    mixed = [OWN + 5, BELOW + 3, ABOVE + 2, ABOVE + 3]
+    lax.fori_loop(0, 5, early, 0)
 
     last = CHUNKS // 2 - 1
     none = [0] * 4
 
     def late(step, _):
-        @pl.when((step == 0) | (step == 3) | (step == 4))
+        @pl.when(step != 1)
         def _():
             @pl.when(step == 0)
             def _():
                 with jax.named_scope("wr0"):
-                    on_own(4)
-                    both(on_ring, 1)
+                    on_own(5)
+                    on_ring(3)
+                    on_own(6)
+                    across_slots(0)
 
             @pl.when(step > 0)
             def _():
                 with jax.named_scope("wr"):
-                    both(on_ring, step - 1)
-                    pl.when(step == 3)(functools.partial(across_slots, 1))
-
-            chunks = zip(around(1), none, none, around(2), around(3))
-            later = zip(pair(OWN, 2) * 2, none, none, around(3), pair(ACROSS, 1) * 2)
+                    @pl.when(step == 2)
+                    def _():
+                        both(on_ring, 2)
+                        across_slots(1)
+
+                    pl.when(step == 3)(functools.partial(on_ring, 7))
+
+            chunks = zip(mixed, none, around(2), around(3))
+            later = zip(pair(ACROSS, 0) * 2, none, pair(ACROSS, 1) * 2, pair(ACROSS, 2) * 2)
             with jax.named_scope("ring"):
                 add([pick(step, *options) for options in chunks], [pick(step, *options) for options in later])
 
-        @pl.when(step != 3)
-        def _():
-            @pl.when(step < 3)
-            def _():
-                with jax.named_scope("wo"):
-                    on_own(5 + step)
-                    pl.when(step == 0)(functools.partial(across_slots, 0))
-                    pl.when(step == 1)(functools.partial(both, on_across, 0))
-
-            @pl.when(step > 3)
-            def _():
-                with jax.named_scope("wa"):
-                    both(on_across, step - 3)
-
-            chunks = zip(pair(OWN, 2), pair(ACROSS, 0), pair(OWN, 3), (0, 0), pair(ACROSS, 1), pair(ACROSS, 2))
-            later = zip(pair(ACROSS, 0) * 2, pair(OWN, 3) * 2, around(2), none, pair(ACROSS, 2) * 2, pair(ACROSS, 3) * 2)
-            with jax.named_scope("single"):
-                add([pick(step, *options) for options in chunks], [pick(step, *options) for options in later])
-
+        @pl.when(step == 0)
+        def _():
+            with jax.named_scope("wa0"):
+                both(on_across, 0)
+
+        @pl.when(step == 1)
+        def _():
+            with jax.named_scope("wo"):
+                on_own(7)
+
+        @pl.when(step > 1)
+        def _():
+            with jax.named_scope("wa"):
+                both(on_across, step - 1)
+                pl.when(step == 2)(functools.partial(on_ring, 6))
+
+        chunks = zip(pair(ACROSS, 0), pair(OWN, 3), pair(ACROSS, 1), pair(ACROSS, 2))
+        later = zip(pair(OWN, 3) * 2, around(2), around(3), pair(ACROSS, 3) * 2)
+        with jax.named_scope("single"):
+            add([pick(step, *options) for options in chunks], [pick(step, *options) for options in later])
         return 0
 
-    lax.fori_loop(0, 6, late, 0)
+    lax.fori_loop(0, 4, late, 0)
     with jax.named_scope("w_last"):
         both(on_across, last)
     with jax.named_scope("last"):
@@ -360,8 +383,8 @@
         left(sent_slots.at[most], send_sem.at[0])
         left(values.at[0, most], send_sem.at[1])
         left(row_slots.at[pl.ds(0, 2 * MEMBERS)], send_sem.at[2])
-        left(rows.at[pl.ds(0, 2 * CHUNKS)], send_sem.at[3])
-        left(rows.at[pl.ds(0, CHUNKS)], send_sem.at[4])
+        left(rows.at[pl.ds(0, 2 * CHUNKS + 1)], send_sem.at[3])
+        left(rows.at[pl.ds(0, CHUNKS - 1)], send_sem.at[4])
         left(row_slots.at[pl.ds(0, MEMBERS)], send_sem.at[5])
         left(values.at[0, most], send_sem.at[6])
     with jax.named_scope("waitback"):

time: 59.8 us -> 59.2 us (0.990)
  Pallas kernels: 59 us -> 58.4 us
    pallas_call x1, Pallas kernels: 56.9 us -> 56.3 us  [per_device(): pl.pallas_call(kernel, out_shape=(jax.ShapeDtypeStruct((BUCKET, BLOCK), j...]
where the time goes in v4:
time: 59.2 us; the launch traced here: 59 us
  Pallas kernels  58.4 us (99%)
  between operations  0.64 us (1%)
    pallas_call x1, Pallas kernels, per_device(): pl.pallas_call(kernel, out_shape=(jax.ShapeDtypeStruct((BUCKET, BLOCK), j...  56.3 us
    pallas_call x1, Pallas kernels, per_device(): pl.pallas_call(hand_over, out_shape=[jax.ShapeDtypeStruct(x.shape, x.dtyp...  2.08 us

profile of v4, /device:TPU:1, one launch (start us, length us, event | category | flops | bytes accessed | tf_op | source)
XLA Modules:
  0.0 59.0 jit_solution(4703702480486628033)
XLA Ops:
  0.6 56.3 %merge.1 = (f32[7168,128]{1,0:T(8,128)S(1)}, bf16[1,64,32,128]{3,2,1,0:T(8,128)(2,1)S(1)}) custom-call(bf16[1,64,32,128]{3,2,1,0:T(8,128)(2,1)} %values_in.1, s32[1,32,64]{2,1,0:T(8,128)} %bitcast.1, s32[1,64]{1,0:T(1,128)} %counts_in.1), custom_call_target="tpu_custom_call" | custom-call | tf_op jit(solution)/shard_map/merge/pallas_call | solution.py:413
  56.9 2.1 %hand_over.1 = (f32[7168,128]{1,0:T(8,128)}, bf16[1,64,32,128]{3,2,1,0:T(8,128)(2,1)}) custom-call(f32[7168,128]{1,0:T(8,128)S(1)} %get-tuple-element.4.averaged, bf16[1,64,32,128]{3,2,1,0:T(8,128)(2,1)S(1)} %get-tuple-element.5.returned), custom_call_target="tpu_custom_call" | custom-call | tf_op jit(solution)/shard_map/hand_over/pallas_call | solution.py:446

commit v5 on v4

--- a/solution.py
+++ b/solution.py
@@ -261,14 +261,15 @@
                 for i in range(1, CHUNKS // 2):
                     both(own_slots, i)
                 pass_slots(1)
-                both(on_own, 1)
+                on_own(2)
                 widen(OWN + 2)
-                widen(OWN + 3)
+            with jax.named_scope("one"):
+                add([OWN + 2], [OWN + 3, OWN + 4])
 
         @pl.when(step == 2)
         def _():
             with jax.named_scope("w2"):
-                on_own(4)
+                on_own(3)
                 ring_slots(0)
                 widen(BELOW)
                 widen(ABOVE)
@@ -277,25 +278,33 @@
         @pl.when(step == 3)
         def _():
             with jax.named_scope("w3"):
+                on_own(4)
+
+        @pl.when(step == 4)
+        def _():
+            with jax.named_scope("w4"):
                 on_ring(1)
                 ring_slots(1)
 
-        @pl.when(step == 4)
-        def _():
-            with jax.named_scope("w4"):
+        @pl.when(step == 5)
+        def _():
+            with jax.named_scope("w5"):
                 on_ring(2)
 
-        chunks = zip(pair(OWN, 0), pair(OWN, 1), (BELOW, ABOVE), (BELOW + 1, ABOVE + 1), (OWN + 4, BELOW + 2))
-        later = zip(pair(OWN, 0) * 2, pair(OWN, 0) * 2, (BELOW + 1, ABOVE + 1) * 2, (OWN + 4, BELOW + 2) * 2, mixed)
-        with jax.named_scope("early"):
-            add([pick(step, *options) for options in chunks], [pick(step, *options) for options in later])
+        @pl.when(step != 1)
+        def _():
+            first, second, third = (BELOW, ABOVE), (BELOW + 1, ABOVE + 1), (BELOW + 2, ABOVE + 2)
+            chunks = zip(pair(OWN, 0), (0, 0), first, (OWN + 3, OWN + 4), second, third)
+            later = zip(pair(OWN, 0) * 2, none, second * 2, second * 2, third * 2, mixed)
+            with jax.named_scope("early"):
+                add([pick(step, *options) for options in chunks], [pick(step, *options) for options in later])
+
         return 0
-
-    mixed = [OWN + 5, BELOW + 3, ABOVE + 2, ABOVE + 3]
-    lax.fori_loop(0, 5, early, 0)
 
     last = CHUNKS // 2 - 1
     none = [0] * 4
+    mixed = [BELOW + 3, ABOVE + 3, OWN + 5, OWN + 6]
+    lax.fori_loop(0, 6, early, 0)
 
     def late(step, _):
         @pl.when(step != 1)
@@ -319,30 +328,33 @@
                     pl.when(step == 3)(functools.partial(on_ring, 7))
 
             chunks = zip(mixed, none, around(2), around(3))
-            later = zip(pair(ACROSS, 0) * 2, none, pair(ACROSS, 1) * 2, pair(ACROSS, 2) * 2)
+            later = zip(pair(ACROSS, 0) + [OWN + 7] * 2, none, pair(ACROSS, 1) * 2, pair(ACROSS, 2) * 2)
             with jax.named_scope("ring"):
                 add([pick(step, *options) for options in chunks], [pick(step, *options) for options in later])
 
-        @pl.when(step == 0)
-        def _():
-            with jax.named_scope("wa0"):
-                both(on_across, 0)
+            @pl.when(step == 0)
+            def _():
+                with jax.named_scope("wa0"):
+                    both(on_across, 0)
+
+            @pl.when(step > 0)
+            def _():
+                with jax.named_scope("wa"):
+                    both(on_across, step - 1)
+                    pl.when(step == 2)(functools.partial(on_ring, 6))
+
+            chunks = zip(pair(ACROSS, 0), (0, 0), pair(ACROSS, 1), pair(ACROSS, 2))
+            later = zip(around(2), none, around(3), pair(ACROSS, 3) * 2)
+            with jax.named_scope("single"):
+                add([pick(step, *options) for options in chunks], [pick(step, *options) for options in later])
 
         @pl.when(step == 1)
         def _():
             with jax.named_scope("wo"):
                 on_own(7)
-
-        @pl.when(step > 1)
-        def _():
-            with jax.named_scope("wa"):
-                both(on_across, step - 1)
-                pl.when(step == 2)(functools.partial(on_ring, 6))
-
-        chunks = zip(pair(ACROSS, 0), pair(OWN, 3), pair(ACROSS, 1), pair(ACROSS, 2))
-        later = zip(pair(OWN, 3) * 2, around(2), around(3), pair(ACROSS, 3) * 2)
-        with jax.named_scope("single"):
-            add([pick(step, *options) for options in chunks], [pick(step, *options) for options in later])
+            with jax.named_scope("one"):
+                add([OWN + 7], [])
+
         return 0
 
     lax.fori_loop(0, 4, late, 0)

time: 59.2 us -> 58.7 us (level)
  no operation moved by 1% of the time
where the time goes in v5:
time: 58.7 us; the launch traced here: 58.5 us
  Pallas kernels  57.9 us (99%)
  between operations  0.64 us (1%)
    pallas_call x1, Pallas kernels, per_device(): pl.pallas_call(kernel, out_shape=(jax.ShapeDtypeStruct((BUCKET, BLOCK), j...  55.8 us
    pallas_call x1, Pallas kernels, per_device(): pl.pallas_call(hand_over, out_shape=[jax.ShapeDtypeStruct(x.shape, x.dtyp...  2.08 us

profile of v5, /device:TPU:1, one launch (start us, length us, event | category | flops | bytes accessed | tf_op | source)
XLA Modules:
  0.0 58.5 jit_solution(4641888536856010472)
XLA Ops:
  0.6 55.8 %merge.1 = (f32[7168,128]{1,0:T(8,128)S(1)}, bf16[1,64,32,128]{3,2,1,0:T(8,128)(2,1)S(1)}) custom-call(bf16[1,64,32,128]{3,2,1,0:T(8,128)(2,1)} %values_in.1, s32[1,32,64]{2,1,0:T(8,128)} %bitcast.1, s32[1,64]{1,0:T(1,128)} %counts_in.1), custom_call_target="tpu_custom_call" | custom-call | tf_op jit(solution)/shard_map/merge/pallas_call | solution.py:425
  56.5 2.1 %hand_over.1 = (f32[7168,128]{1,0:T(8,128)}, bf16[1,64,32,128]{3,2,1,0:T(8,128)(2,1)}) custom-call(f32[7168,128]{1,0:T(8,128)S(1)} %get-tuple-element.4.averaged, bf16[1,64,32,128]{3,2,1,0:T(8,128)(2,1)S(1)} %get-tuple-element.5.returned), custom_call_target="tpu_custom_call" | custom-call | tf_op jit(solution)/shard_map/hand_over/pallas_call | solution.py:458

commit v6 on v5

--- a/solution.py
+++ b/solution.py
@@ -322,7 +322,7 @@
                 with jax.named_scope("wr"):
                     @pl.when(step == 2)
                     def _():
-                        both(on_ring, 2)
+                        on_ring(5)
                         across_slots(1)
 
                     pl.when(step == 3)(functools.partial(on_ring, 7))
@@ -351,6 +351,7 @@
         @pl.when(step == 1)
         def _():
             with jax.named_scope("wo"):
+                on_ring(4)
                 on_own(7)
             with jax.named_scope("one"):
                 add([OWN + 7], [])

time: 58.7 us -> 58.7 us (level)
  no operation moved by 1% of the time
where the time goes in v6:
time: 58.7 us; the launch traced here: 58.5 us
  Pallas kernels  57.9 us (99%)
  between operations  0.64 us (1%)
    pallas_call x1, Pallas kernels, per_device(): pl.pallas_call(kernel, out_shape=(jax.ShapeDtypeStruct((BUCKET, BLOCK), j...  55.8 us
    pallas_call x1, Pallas kernels, per_device(): pl.pallas_call(hand_over, out_shape=[jax.ShapeDtypeStruct(x.shape, x.dtyp...  2.08 us

profile of v6, /device:TPU:1, one launch (start us, length us, event | category | flops | bytes accessed | tf_op | source)
XLA Modules:
  0.0 58.5 jit_solution(15292427472300759131)
XLA Ops:
  0.6 55.8 %merge.1 = (f32[7168,128]{1,0:T(8,128)S(1)}, bf16[1,64,32,128]{3,2,1,0:T(8,128)(2,1)S(1)}) custom-call(bf16[1,64,32,128]{3,2,1,0:T(8,128)(2,1)} %values_in.1, s32[1,32,64]{2,1,0:T(8,128)} %bitcast.1, s32[1,64]{1,0:T(1,128)} %counts_in.1), custom_call_target="tpu_custom_call" | custom-call | tf_op jit(solution)/shard_map/merge/pallas_call | solution.py:426
  56.4 2.1 %hand_over.1 = (f32[7168,128]{1,0:T(8,128)}, bf16[1,64,32,128]{3,2,1,0:T(8,128)(2,1)}) custom-call(f32[7168,128]{1,0:T(8,128)S(1)} %get-tuple-element.4.averaged, bf16[1,64,32,128]{3,2,1,0:T(8,128)(2,1)S(1)} %get-tuple-element.5.returned), custom_call_target="tpu_custom_call" | custom-call | tf_op jit(solution)/shard_map/hand_over/pallas_call | solution.py:459
